TPU v7x, 64 devices: a 2x2x8 block of a 4x4x8 slice. The times are simulated.
64 devices in a mesh: dp: 4 (over x, y), tp: 16 (over z, core).
Axes of the slice: x: 2, y: 2, z: 8, core: 2. Of those that a mesh axis runs over, the one named last changes fastest.
The devices are a block of a 4x4x8 slice.
Arguments:
- tok_ids: int32 [16, 512], P('dp'), parts along dimension 0
- embed: bfloat16 [2048, 4096], P('tp')
- norm_gain: float32 [4096], replicated
- q_gain: float32 [128], replicated
- k_gain: float32 [128], replicated
- w_query: bfloat16 [4096, 8192], P(None, 'tp')
- w_key: bfloat16 [4096, 512], P(None, 'tp')
- w_value: bfloat16 [4096, 512], P(None, 'tp')
- w_out: bfloat16 [8192, 4096], P('tp')
- grad_y: bfloat16 [16, 512, 4096], P('dp', 'tp'), parts along dimension 0
Outputs:
- output 1: bfloat16 [16, 512, 4096], P('dp', 'tp'), parts along dimension 0
- output 2: float32 [8192, 4096], P(('dp', 'tp')), parts along dimension 0
- output 3: float32 [16384], P('dp'), parts along dimension 0
- output 4: float32 [512], P('dp'), parts along dimension 0
- output 5: float32 [512], P('dp'), parts along dimension 0
- output 6: float32 [16384, 8192], P('dp', 'tp'), parts along dimension 0
- output 7: float32 [16384, 512], P('dp', 'tp'), parts along dimension 0
- output 8: float32 [16384, 512], P('dp', 'tp'), parts along dimension 0
- output 9: float32 [32768, 4096], P(('dp', 'tp')), parts along dimension 0
There are 4 independent parts. A program takes and returns all parts, laid end to end along the dimension named above; an argument that names none is the same for every part.
All inputs are finite; a program needn't handle non-finite values.
Results may differ from a plain program's by a relative error of at most 0.02.
Values are sent between devices in bfloat16 or wider.
A program may use at most 768 MiB of HBM per device.

v0:
```python
import functools
import jax
import jax.numpy as jnp
import numpy as np
from jax import lax
from jax.experimental import pallas as pl
from jax.experimental.pallas import tpu as pltpu
from jax.sharding import PartitionSpec as P

BF = jnp.bfloat16
F32 = jnp.float32
EPS = 1.0e-6
ROPE_BASE = 1.0e6
NEG_BIG = -1.0e30
LOG2E = 1.4426950408889634
MESH = pl.DeviceIdType.MESH
ANY = pl.BlockSpec(memory_space=pl.ANY)
VM = pl.BlockSpec(memory_space=pltpu.VMEM)
NT = (((1,), (1,)), ((), ()))
NN = (((1,), (0,)), ((), ()))
TN = (((0,), (0,)), ((), ()))


def dotf(a, b, dims=NN):
    return lax.dot_general(a, b, dims, preferred_element_type=F32)


def rdma(src, dst, ssem, rsem, dev):
    return pltpu.make_async_remote_copy(src_ref=src, dst_ref=dst, send_sem=ssem, recv_sem=rsem, device_id={'tp': dev}, device_id_type=MESH)


def span(start, size):
    return pl.ds(pl.multiple_of(start, size), size)


def each(lo, hi, f):
    def go(j, _):
        f(j)
        return 0
    lax.fori_loop(lo, hi, go, 0)


def total(ref, sem):
    pltpu.make_async_copy(ref, ref, sem).wait()


def rms_f32(x, gain):
    return x * lax.rsqrt(jnp.mean(x * x, axis=-1, keepdims=True) + EPS) * gain


def rms_pull(x, dxr, r):
    return r * dxr - x * (r * r * r * jnp.mean(x * dxr, axis=-1, keepdims=True))


def causal_blocks(q, keys, i, blk):
    r_i = lax.broadcasted_iota(jnp.int32, (blk, blk), 0)
    c_i = lax.broadcasted_iota(jnp.int32, (blk, blk), 1)
    s = [dotf(q, keys[j * blk:(j + 1) * blk], NT) for j in range(i + 1)]
    s[i] = jnp.where(r_i >= c_i, s[i], NEG_BIG)
    top = functools.reduce(jnp.maximum, [jnp.max(t, axis=-1, keepdims=True) for t in s])
    c = q.shape[-1] ** -0.5 * LOG2E
    e = [jnp.exp2((t - top) * c) for t in s]
    inv = 1.0 / sum(jnp.sum(t, axis=-1, keepdims=True) for t in e)
    return [t * inv for t in e]


def body(nz, embed, gy, wq, wk_t, wv_t, wo, gain, qg, kg, cos, sin_s, tok_seq,
         y_hbm, ge_hbm, gq_hbm, gk_hbm, gv_hbm, gwo_hbm, gn_out, gqg_out, gkg_out, erows, hid, gy_out, wqt_out, wqts_out, py_out, ph_out,
         table, wpair, wq_v, qt, o_own, o_sib, sq, kv_tok, k_rot, kvacc, farkv, kvrow, skv, kvc, d_rows, pbuf, hbuf, gown, hotm,
         dk_acc, dv_acc, pk, rk1, fk, hk, rk2, kvt, gn, qga, kga, gmine, gsib, gcol, gfin, y_v, ge_v, gkv_v,
         in_sem, h_sem, g_sem, r_sem, s_sem, a_s, b_s, xs, xr, wq_s, wq_r, w_s, o_s, pt_sem, pl_sem, rs, p1s, p1r, p2s, p2r, qs, gls, hls, swos, swqs, gs, out_sem, e_sem):
    rank = lax.axis_index('tp')
    z, core = rank // 2, lax.rem(rank, 2)
    right = 2 * lax.rem(z + 1, nz) + core
    left = 2 * lax.rem(z + nz - 1, nz) + core
    sib = rank + 1 - 2 * core
    par = lax.rem(z, 2)
    far = rank + 2 - 4 * par
    vrows, d = embed.shape
    kn = wk_t.shape[0]
    sub_rows = vrows // 4
    vocab = vrows * 2 * nz
    vhalf = vocab // 2
    batch, seq = tok_seq.shape
    toks = batch * seq
    qn = wq.shape[1]
    hd = qg.shape[1]
    heads = qn // hd
    events = 2 * nz
    pos = seq // events
    blk = seq // 2
    bw = d // events
    scale = hd ** -0.5
    units = batch * heads
    parts = 8
    wo_p, wq_p = qn // parts, d // parts
    both = (0, 1)
    places = [(dr, c) for dr in both for c in both]
    qr = wq_v.at[pl.ds(0, toks)]
    gd = wq_v.at[pl.ds(toks, toks)]
    w_q = wq_v.at[pl.ds(0, d)]

    ld = [pltpu.make_async_copy(s, t, in_sem.at[i]) for i, (s, t) in enumerate((
        (embed, table.at[span(rank * vrows, vrows)]), (gy, gown), (wq, w_q), (wo, wpair.at[pl.ds(0, qn)]),
        (wk_t, wpair.at[pl.ds(2 * qn, kn)]), (wv_t, wpair.at[pl.ds(2 * qn + kn, kn)])))]
    ld2 = [pltpu.make_async_copy(s, t, in_sem.at[i]) for i, (s, t) in enumerate((
        (wqt_out, wpair.at[pl.ds(0, qn)]), (wqts_out, wpair.at[pl.ds(qn, qn)]), (embed, gown)))]
    ld[0].start()
    barrier = pltpu.get_barrier_semaphore()
    for dev in (right, left, sib):
        pl.semaphore_signal(barrier, inc=1, device_id={'tp': dev}, device_id_type=MESH)
    pl.semaphore_wait(barrier, 3)
    ld[0].wait()

    def nbr(dr):
        return right if dr == 0 else left

    def arrived(sem):
        total(table.at[pl.ds(0, 2 * sub_rows)], sem)

    def zd_of(dr, e):
        s = e // 2
        return lax.rem(z + (nz - s if dr == 0 else s), nz)

    def row_of(dr, e, c):
        return pl.multiple_of(vrows * (2 * zd_of(dr, e) + c) + sub_rows * (2 * dr + lax.rem(e, 2)), sub_rows)

    def ring(dr, e, recv_e):
        a = table.at[pl.ds(row_of(dr, e, core), sub_rows)]
        return rdma(a, a, a_s.at[0], r_sem.at[recv_e], nbr(dr))

    def side(dr, e):
        a = table.at[pl.ds(row_of(dr, e, core), sub_rows)]
        return rdma(a, a, a_s.at[1], s_sem.at[e], sib)

    def e_keep(dr, e):
        dst = pl.multiple_of(vrows * lax.rem(e // 2 + nz - 1, nz) + sub_rows * (2 * dr + lax.rem(e, 2)), sub_rows)
        return pltpu.make_async_copy(table.at[pl.ds(row_of(dr, e, core), sub_rows)], erows.at[pl.ds(dst, sub_rows)], e_sem.at[0])

    def h_copy(slot, i, row):
        return pltpu.make_async_copy(hbuf.at[slot, pl.ds(i * sub_rows, sub_rows)], hid.at[pl.ds(row, sub_rows)], h_sem.at[slot])

    def g_row(dr, e, c):
        return pl.multiple_of(seq * (2 * dr + lax.rem(e, 2)) + pos * (2 * zd_of(dr, e) + c), pos)

    def g_piece(dr, e, c):
        return gy_out.at[pl.ds(g_row(dr, e, c), pos)]

    def g_own(dr, e):
        return gown.at[span(pos * (2 * dr + lax.rem(e, 2)), pos)]

    def g_ring(dr, e, recv_e, first):
        a = g_piece(dr, e, core)
        return rdma(g_own(dr, e) if first else a, a, b_s.at[0 if first else 1], r_sem.at[recv_e], nbr(dr))

    def g_side(dr, e, first):
        a = g_piece(dr, e, core)
        return rdma(g_own(dr, e) if first else a, a, b_s.at[2 if first else 3], s_sem.at[e], sib)

    def g_home(dr, e):
        return pltpu.make_async_copy(g_own(dr, e), g_piece(dr, e, core), in_sem.at[8 + 2 * dr + e])

    def g_fetch(slot, i, dr, c, e):
        return pltpu.make_async_copy(g_piece(dr, e, c), hbuf.at[slot, pl.ds(i * pos, pos)], g_sem.at[0])

    def wo_push(k):
        return rdma(wpair.at[span(k * wo_p, wo_p)], wpair.at[pl.ds(pl.multiple_of(qn + k * wo_p, wo_p), wo_p)], w_s.at[0], w_s.at[1], sib)

    def tb(k):
        return o_own.at[span(lax.rem(k, 2) * qn, qn), pl.ds(0, wq_p)]

    def wq_push(k):
        return rdma(tb(k), wqts_out.at[:, span(k * wq_p, wq_p)], wq_s.at[0, lax.rem(k, 2)], wq_r.at[0], sib)

    def wq_home(k):
        return pltpu.make_async_copy(tb(k), wqt_out.at[:, span(k * wq_p, wq_p)], wq_s.at[1, lax.rem(k, 2)])

    def wk_push(k):
        return rdma((wk_t, wv_t)[k], wpair.at[pl.ds(2 * qn + (2 + k) * kn, kn)], w_s.at[2], w_s.at[3], sib)

    def o_push(b, k):
        src = pl.multiple_of(b * seq + pos * (2 * k + 1 - core), pos)
        dst = pl.multiple_of(vrows * k + pos * b, pos)
        return rdma(o_own.at[pl.ds(src, pos)], o_sib.at[pl.ds(dst, pos)], o_s.at[0], o_s.at[1], sib)

    def project(e):
        slot = lax.rem(e, 2)

        @pl.when(e >= 2)
        def _():
            total(hbuf.at[slot], h_sem.at[slot])

        rows = [row_of(dr, e, c) for dr, c in places]
        for i, row in enumerate(rows):
            x = table[pl.ds(row, sub_rows), :].astype(F32)
            ids = row + lax.broadcasted_iota(jnp.int32, (sub_rows, seq), 0)
            hit = jnp.zeros((sub_rows, seq), F32)
            for b in range(batch):
                hit = jnp.maximum(hit, jnp.where(tok_seq[b:b + 1, :] == ids, 1.0, 0.0))
            used = jnp.max(hit, axis=1, keepdims=True)
            h = jnp.where(used > 0.5, rms_f32(x, gain[...]), 0.0)
            hbuf[slot, pl.ds(i * sub_rows, sub_rows), :] = h.astype(BF)
            h_copy(slot, i, row).start()
        hb = hbuf[slot]
        qkv = jnp.concatenate([dotf(hb, w_q[...]).astype(BF), dotf(hb, wpair[2 * qn:2 * qn + 4 * kn, :], NT).astype(BF)], axis=1)
        lane = lax.broadcasted_iota(jnp.int32, (1, vrows), 1)
        rowid = jnp.zeros((1, vrows), jnp.int32)
        for i, row in enumerate(rows):
            rowid = jnp.where(lane // sub_rows == i, row + lane - i * sub_rows, rowid)
        rowid = rowid.astype(F32)
        for b in range(batch):
            sl = slice(b * seq, (b + 1) * seq)
            hot = jnp.where(d_rows[sl, :vrows] == rowid, 1.0, 0.0).astype(BF)
            got = dotf(hot, qkv)
            qt[sl, :] = (qt[sl, :].astype(F32) + got[:, :qn]).astype(BF)
            at = slice((b % 2) * seq, (b % 2 + 1) * seq)
            kvacc[b // 2, at, :] = (kvacc[b // 2, at, :].astype(F32) + got[:, qn:]).astype(BF)

    def step_a(e):
        @pl.when((e >= 2) & (e < events))
        def _():
            arrived(r_sem.at[e])

        @pl.when(e < events - 2)
        def _():
            for dr in both:
                ring(dr, e, e + 2).start()

        @pl.when(e < events)
        def _():
            for dr in both:
                side(dr, e).start()
                e_keep(dr, e).start()

        @pl.when(e == 0)
        def _():
            for c in ld[1:]:
                c.start()
            for k in both:
                wk_push(k).start()
            for b in range(batch):
                wide = jnp.broadcast_to(tok_seq[b:b + 1, :].astype(F32), (vrows, seq))
                d_rows[b * seq:(b + 1) * seq, :vrows] = wide.T
            qt[...] = jnp.zeros_like(qt)
            kvacc[...] = jnp.zeros_like(kvacc)

        @pl.when(e == 1)
        def _():
            for c in ld[1:]:
                c.wait()
            total(wpair.at[pl.ds(2 * qn, 2 * kn)], w_s.at[3])
            for dr in both:
                for k in both:
                    g_home(dr, k).start()

        @pl.when((e >= events - 2) & (e < events))
        def _():
            for dr in both:
                g_ring(dr, e - events + 2, e - events + 4, True).start()

        @pl.when((e >= 2) & (e < 4 + parts))
        def _():
            @pl.when(e >= 4)
            def _():
                wq_push(e - 4).wait_send()
                wq_home(e - 4).wait()

            @pl.when(e < 2 + parts)
            def _():
                k = e - 2
                block = wq_v[span(k * wq_p, wq_p), :]
                tb(k)[...] = block.astype(F32).T.astype(BF)
                wo_push(k).start()
                wq_push(k).start()
                wq_home(k).start()

        @pl.when(e >= 1)
        def _():
            arrived(s_sem.at[e - 1])
            project(e - 1)

    each(0, events + 1, step_a)

    to_far = rdma(kvacc.at[core], farkv.at[core], xs.at[0], xr.at[0], far)
    relay = rdma(farkv.at[core], farkv.at[core], xs.at[1], xr.at[1], sib)
    at_i = lax.broadcasted_iota(jnp.int32, (pos, seq), 1) - pos * rank
    own_i = lax.broadcasted_iota(jnp.int32, (pos, seq), 0)
    col = jnp.concatenate([jnp.sum(jnp.where(at_i == own_i, tok_seq[b:b + 1, :].astype(F32), 0.0), axis=1, keepdims=True) for b in range(batch)], axis=0).astype(jnp.int32)
    lanes = lax.broadcasted_iota(jnp.int32, (vrows, vrows), 1)
    hot_mine = jnp.concatenate([jnp.where(col == lanes + j * vrows, 1.0, 0.0).astype(BF) for j in range(vocab // vrows)], axis=1)
    to_far.start()
    for dr in both:
        for k in both:
            g_side(dr, k, True).start()
            g_home(dr, k).wait()
    cw = min(512, d)

    def own_rows(j):
        y_v[:, span(j * cw, cw)] = dotf(hot_mine, table[:, span(j * cw, cw)]).astype(BF)

    each(0, d // cw, own_rows)
    for b in range(batch):
        ids = rank * vrows + lax.broadcasted_iota(jnp.int32, (vrows, seq), 0)
        hotm[:, b * seq:(b + 1) * seq] = jnp.where(ids == tok_seq[b:b + 1, :], 1.0, 0.0).astype(BF)

    def place(p, first):
        l_i = lax.broadcasted_iota(jnp.int32, (4 * kn, 2 * hd), 0)
        m_i = lax.broadcasted_iota(jnp.int32, (4 * kn, 2 * hd), 1)
        upper = jnp.where(l_i >= 2 * kn, 1, 0)
        owner = jnp.where(upper == 1, 1 - first, first)
        l_i = l_i - 2 * kn * upper
        base = kn * (2 * p + owner)
        want = jnp.where(l_i < kn, base + l_i, hd + base + l_i - kn)
        return jnp.where(m_i == want, 1.0, 0.0).astype(BF)

    def rope(raw, g):
        n = rms_f32(raw.astype(F32), g)
        return (n * cos[...] + pltpu.roll(n, hd // 2, 1) * sin_s[...]).astype(BF)

    def attend(u):
        base = (u // heads) * seq
        rows = span(base, seq)
        cols = span(lax.rem(u, heads) * hd, hd)
        q = rope(qt[rows, cols], qg[...])
        qr[rows, cols] = q
        kr = k_rot[rows, :]
        v = kv_tok[rows, hd:]
        for i in both:
            p = causal_blocks(q[i * blk:(i + 1) * blk], kr, i, blk)
            o = sum(dotf(t.astype(BF), v[j * blk:(j + 1) * blk]) for j, t in enumerate(p))
            o_own[pl.ds(pl.multiple_of(base + i * blk, blk), blk), cols] = o.astype(BF)

    def grad_attend(e):
        total(hbuf, g_sem.at[0])
        r = dotf(hbuf[...].reshape(2 * vrows, d), wpair[:qn, :], NT).astype(BF)
        for k in both:
            for i, (dr, c) in enumerate(places):
                n = (4 * k + i) * pos
                gd[pl.ds(g_row(dr, e + k, c), pos), :] = r[n:n + pos]

    def pstage(j):
        return d_rows.at[span(lax.rem(j, 2) * vhalf, vhalf), pl.ds(0, bw)]

    def pstore(dst, j):
        return pltpu.make_async_copy(pstage(j), dst.at[:, span(j * bw, bw)], pt_sem.at[lax.rem(j, 2)])

    def pblock(dst, j, pairs):
        @pl.when(j >= 2)
        def _():
            pstore(dst, j - 2).wait()
        cols = span(j * bw, bw)
        acc = None
        for a, lo, n in pairs:
            t = dotf(a[...], wpair[lo:lo + n, cols])
            acc = t if acc is None else acc + t
        pstage(j)[...] = acc
        pstore(dst, j).start()

    y_pairs = [(sq, 0, qn), (o_sib, qn, qn)]

    def pslot(ph, e, dr):
        return pbuf.at[2 * ph + lax.rem(e, 2), dr]

    def pfetch(ph, e, dr):
        s = e // 2
        step = s if ph else lax.rem(z + (2 * nz - 1 - s if dr == 0 else 1 + s), nz)
        row = pl.multiple_of(vrows * step + sub_rows * (2 * dr + lax.rem(e, 2)), sub_rows)
        return pltpu.make_async_copy((py_out, ph_out)[ph].at[pl.ds(row, sub_rows)], pslot(ph, e, dr), pl_sem.at[ph, lax.rem(e, 2)])

    def item(i):
        row = vrows * (i // 2)
        cps = []
        for dr in both:
            at = pl.ds(pl.multiple_of(row + sub_rows * (2 * dr + lax.rem(i, 2)), sub_rows), sub_rows)
            cps.append(pltpu.make_async_copy(ph_out.at[at], pbuf.at[lax.rem(i, 2), dr], pl_sem.at[0, lax.rem(i, 2)]))
            cps.append(pltpu.make_async_copy(erows.at[at], hbuf.at[lax.rem(i, 2), pl.ds(dr * sub_rows, sub_rows)], e_sem.at[1 + lax.rem(i, 2)]))
        return cps

    def gain_part(i):
        total(pbuf.at[lax.rem(i, 2)], pl_sem.at[0, lax.rem(i, 2)])
        total(hbuf.at[lax.rem(i, 2), pl.ds(0, 2 * sub_rows)], e_sem.at[1 + lax.rem(i, 2)])
        for dr in both:
            x = hbuf[lax.rem(i, 2), dr * sub_rows:(dr + 1) * sub_rows, :].astype(F32)
            t = pbuf[lax.rem(i, 2), dr] * (x * lax.rsqrt(jnp.mean(x * x, axis=-1, keepdims=True) + EPS))
            gn[...] += sum(t[k:k + 8] for k in range(0, sub_rows, 8))

        @pl.when(i + 2 < events)
        def _():
            for c in item(i + 2):
                c.start()

    def fetched(ph, e):
        total(pbuf.at[2 * ph + lax.rem(e, 2)], pl_sem.at[ph, lax.rem(e, 2)])

    def rslot(dr, e):
        return table.at[span((dr * (events - 2) + e) * sub_rows, sub_rows)]

    def sslot(ph, dr, e):
        k = 2 * (events - 2) + 8 * ph + 4 * lax.rem(e // 2, 2) + 2 * dr + lax.rem(e, 2)
        return table.at[span(k * sub_rows, sub_rows)]

    def send(ph, dr, e):
        return rdma(sslot(ph, dr, e), rslot(dr, e), rs.at[ph, lax.rem(e, 4)], r_sem.at[e + 2], nbr(dr))

    def first_fetch(ph):
        for e in both:
            for dr in both:
                pfetch(ph, e, dr).start()

    def first_sends(ph):
        for e in both:
            fetched(ph, e)
            for dr in both:
                sslot(ph, dr, e)[...] = pslot(ph, e, dr)[...].astype(BF)
        for e in both:
            for dr in both:
                send(ph, dr, e).start()
                pfetch(ph, e + 2, dr).start()

    def serve(ph, e, final):
        arrived(r_sem.at[e])
        fetched(ph, e)

        @pl.when(e < events - 2)
        def _():
            @pl.when(e >= 4)
            def _():
                arrived(rs.at[ph, lax.rem(e, 4)])
            for dr in both:
                sslot(ph, dr, e)[...] = (pslot(ph, e, dr)[...] + rslot(dr, e - 2)[...].astype(F32)).astype(BF)
            for dr in both:
                send(ph, dr, e).start()
                pfetch(ph, e + 2, dr).start()

        @pl.when(e >= events - 2)
        def _():
            for dr in both:
                final(dr, lax.rem(e, 2), pslot(ph, e, dr)[...] + rslot(dr, e - 2)[...].astype(F32))

    slots = 9

    def gather_o(k):
        for b in range(batch):
            src = pl.multiple_of(b * seq + pos * (2 * k + core), pos)
            sq[pl.ds(pl.multiple_of(vrows * k + pos * b, pos), pos), :] = o_own[pl.ds(src, pos), :]

    def upto(e, n, over):
        return jnp.minimum((e * n) // over, n)

    def step_b(e):
        @pl.when(e == events - 2)
        def _():
            first_sends(0)

        @pl.when((e >= 2) & (e < events))
        def _():
            arrived(r_sem.at[e])

        @pl.when((e >= 2) & (e < events - 2))
        def _():
            for dr in both:
                g_ring(dr, e, e + 2, False).start()

        @pl.when((e >= 2) & (e < events))
        def _():
            for dr in both:
                g_side(dr, e, False).start()

        @pl.when((e >= 1) & (e <= events))
        def _():
            arrived(s_sem.at[e - 1])

        @pl.when(e == 2)
        def _():
            to_far.wait_recv()
            relay.start()

        @pl.when(e == 3)
        def _():
            rdma(farkv.at[1 - core], farkv.at[1 - core], xs.at[1], xr.at[1], sib).wait_recv()
            for hf in both:
                kv_tok[hf * (toks // 2):(hf + 1) * (toks // 2), :] = (dotf(kvacc[hf], place(par, core)) + dotf(farkv[hf], place(1 - par, hf))).astype(BF)
            for b in range(batch):
                sl = slice(b * seq, (b + 1) * seq)
                k_rot[sl, :] = rope(kv_tok[sl, :hd], kg[...])

        @pl.when((e >= 2) & (lax.rem(e, 2) == 0))
        def _():
            for k in both:
                for i, (dr, c) in enumerate(places):
                    g_fetch(k, i, dr, c, e - 2 + k).start()

        def give(b):
            each(0, nz, lambda k: o_push(b, k).start())

        def seen(t):
            return jnp.minimum((jnp.maximum(t - 3, 0) * units) // (slots - 3), units)

        each(seen(e - 1) // heads, seen(e) // heads, give)
        each(seen(e), seen(e + 1), attend)

        @pl.when(e == 4)
        def _():
            total(table.at[pl.ds(0, 2 * (events - 2) * sub_rows)], a_s.at[0])
            total(table.at[pl.ds(0, 2 * events * sub_rows)], a_s.at[1])
            total(erows, e_sem.at[0])

        @pl.when(e == slots + 1)
        def _():
            total(wpair.at[pl.ds(0, qn)], w_s.at[1])
            total(o_sib, o_s.at[1])
            each(0, nz, gather_o)

        @pl.when((e > slots) & (e <= slots + 4))
        def _():
            each(4 * (e - slots - 1), 4 * (e - slots), lambda j: pblock(py_out, j, y_pairs))

        @pl.when(e == slots + 4)
        def _():
            for j in (events - 2, events - 1):
                pstore(py_out, j).wait()
            first_fetch(0)

        @pl.when((e >= 3) & (lax.rem(e, 2) == 1))
        def _():
            grad_attend(e - 3)

    for slot in both:
        total(hbuf.at[slot], h_sem.at[slot])
    each(0, events + 2, step_b)

    def pull(raw, dout, g):
        x = raw.astype(F32)
        r = lax.rsqrt(jnp.mean(x * x, axis=-1, keepdims=True) + EPS)
        dn = dout * cos[...] + pltpu.roll(dout * sin_s[...], hd // 2, 1)
        return rms_pull(x, dn * g, r).astype(BF), jnp.sum(dn * (x * r), axis=0, keepdims=True)

    def unit(u):
        b, h = u // heads, lax.rem(u, heads)
        rows = span(b * seq, seq)
        cols = span(h * hd, hd)

        @pl.when(h == 0)
        def _():
            dk_acc[...] = jnp.zeros_like(dk_acc)
            dv_acc[...] = jnp.zeros_like(dv_acc)
        q, g = qr[rows, cols], gd[rows, cols]
        kr, v = k_rot[rows, :], kv_tok[rows, hd:]
        dqs = []
        for i in both:
            qi, gi = q[i * blk:(i + 1) * blk], g[i * blk:(i + 1) * blk]
            p = causal_blocks(qi, kr, i, blk)
            dp = [dotf(gi, v[j * blk:(j + 1) * blk], NT) for j in range(i + 1)]
            tot = sum(jnp.sum(a * b, axis=-1, keepdims=True) for a, b in zip(p, dp))
            dq = None
            for j in range(i + 1):
                at = slice(j * blk, (j + 1) * blk)
                dv_acc[at, :] += dotf(p[j].astype(BF), gi, TN)
                ds = (p[j] * (dp[j] - tot)).astype(BF)
                t = dotf(ds, kr[at])
                dq = t if dq is None else dq + t
                dk_acc[at, :] += dotf(ds, qi, TN)
            dqs.append(dq * scale)
        dq = jnp.concatenate(dqs, axis=0).astype(BF).astype(F32)
        dx, dg = pull(qt[rows, cols], dq, qg[...])
        gd[rows, cols] = dx
        qga[...] += dg

    def pick(r, up):
        m_i = lax.broadcasted_iota(jnp.int32, (2 * hd, 4 * kn), 0)
        l_i = lax.broadcasted_iota(jnp.int32, (2 * hd, 4 * kn), 1) - 2 * kn * up
        is_k = (l_i >= 0) & (l_i < kn) & (m_i == l_i + kn * r)
        is_v = (l_i >= kn) & (l_i < 2 * kn) & (m_i == hd + kn * r + l_i - kn)
        return jnp.where(is_k | is_v, 1.0, 0.0).astype(BF)

    def to_side(b, p):
        return rdma(pk.at[b, 2 * p + 1 - core], rk1.at[b, p], p1s.at[0], p1r.at[b], sib)

    def to_far2(b):
        return rdma(fk.at[b], rk2.at[b], p2s.at[0], p2r.at[b], far)

    def kv_one(b):
        dk = (dk_acc[...] * scale).astype(BF).astype(F32)
        dx, dg = pull(kv_tok[span(b * seq, seq), :hd], dk, kg[...])
        kga[...] += dg
        gkv = jnp.concatenate([dx, dv_acc[...].astype(BF)], axis=1)
        for r in range(4):
            pk[b, r] = (dotf(gkv[:blk], pick(r, 0)) + dotf(gkv[blk:], pick(r, 1))).astype(BF)
        for p in both:
            to_side(b, p).start()

    def kv_two(b):
        total(rk1.at[b], p1r.at[b])
        fk[b] = (pk[b, 2 * (1 - par) + core].astype(F32) + rk1[b, 1 - par].astype(F32)).astype(BF)
        hk[b] = pk[b, 2 * par + core].astype(F32) + rk1[b, par].astype(F32)
        to_far2(b).start()

    def kv_three(b):
        to_far2(b).wait_recv()
        t = hk[b] + rk2[b].astype(F32)
        low = lax.broadcasted_iota(jnp.int32, t.shape, 1) < 2 * kn
        kvt[b, :blk, :] = jnp.where(low, t, 0.0).astype(BF)
        kvt[b, blk:, :] = jnp.where(low, pltpu.roll(t, 2 * kn, 1), 0.0).astype(BF)

    def fold(b, tile):
        rows = span(tile * seq, seq)
        ids = tile * seq + lax.broadcasted_iota(jnp.int32, (seq, seq), 0)
        hot = jnp.where(ids == tok_seq[pl.ds(b, 1), :], 1.0, 0.0).astype(BF)
        d_rows[rows, :qn] += dotf(hot, gd[span(b * seq, seq), :])
        d_rows[rows, qn:] += dotf(hot, kvt[b])

    tiles = vocab // seq

    def run_unit(u):
        unit(u)

        @pl.when(lax.rem(u, heads) == heads - 1)
        def _():
            kv_one(u // heads)

        @pl.when((u >= heads) & (lax.rem(u, heads) == 1))
        def _():
            kv_two(u // heads - 1)

    def run_fold(f):
        b, tile = f // tiles, lax.rem(f, tiles)

        @pl.when(tile == 0)
        def _():
            kv_three(b)
        fold(b, tile)

    def share(e, first, n, over):
        return jnp.minimum((jnp.maximum(e - first, 0) * n) // over, n)

    def paced(e, first, n, over, f):
        each(share(e, first, n, over), share(e + 1, first, n, over), f)

    def settle(t):
        rows = span(t * vrows, vrows)
        qt[rows, :] = d_rows[rows, :qn].astype(BF)
        kvrow[rows, :] = d_rows[rows, qn:].astype(BF)

    def step_row(k, dr):
        return pl.multiple_of(vrows * lax.rem(z + nz - 1 - k if dr == 0 else k + nz - 1 - z, nz) + 2 * sub_rows * dr, 2 * sub_rows)

    def swap(k, dr, kk):
        src = pl.multiple_of(vrows * (2 * k + 1 - core) + 2 * sub_rows * dr, 2 * sub_rows)
        return rdma((qt, kvrow)[kk].at[pl.ds(src, 2 * sub_rows)], (sq, skv)[kk].at[pl.ds(step_row(k, dr), 2 * sub_rows)], qs.at[0, kk], qs.at[1, kk], sib)

    def gather_h(k):
        for dr in both:
            src = pl.multiple_of(vrows * (2 * k + core) + 2 * sub_rows * dr, 2 * sub_rows)
            dst = pl.ds(step_row(k, dr), 2 * sub_rows)
            o_sib[dst, :] = qt[pl.ds(src, 2 * sub_rows), :]
            kvc[dst, :] = (kvrow[pl.ds(src, 2 * sub_rows), :].astype(F32) + pltpu.roll(skv[dst, :].astype(F32), 2 * kn, 1)).astype(BF)

    hrows = vhalf // 2

    def hstage(j):
        return d_rows.at[pl.ds(pl.multiple_of(vhalf + lax.rem(j, 2) * hrows, hrows), hrows), pl.ds(0, bw)]

    def hstore(j):
        return pltpu.make_async_copy(hstage(j), ph_out.at[span((j // events) * hrows, hrows), span(lax.rem(j, events) * bw, bw)], pt_sem.at[lax.rem(j, 2)])

    def hblock(j):
        @pl.when(lax.rem(j, events) >= 2)
        def _():
            hstore(j - 2).wait()
        rows = span((j // events) * hrows, hrows)
        cols = span(lax.rem(j, events) * bw, bw)
        hstage(j)[...] = dotf(o_sib[rows, :], wpair[:qn, cols]) + dotf(sq[rows, :], wpair[qn:2 * qn, cols]) + dotf(kvc[rows, :], wpair[2 * qn:2 * qn + 4 * kn, cols])
        hstore(j).start()

    def final_y(dr, sub, acc):
        rows = span((2 * dr + sub) * pos, pos)
        y_v[rows, :] = (y_v[rows, :].astype(F32) + acc).astype(BF)

    def step_c(e):
        @pl.when(e == events - 2)
        def _():
            first_sends(1)

        @pl.when(e >= 2)
        def _():
            serve(0, e, final_y)

        @pl.when(e == 0)
        def _():
            total(gown, b_s.at[0])
            total(gown, b_s.at[2])
            total(wqts_out, wq_r.at[0])
            total(wpair.at[pl.ds(0, qn)], w_s.at[0])
            for c in ld2:
                c.start()
            d_rows[...] = jnp.zeros_like(d_rows)
            gn[...] = jnp.zeros_like(gn)
            qga[...] = jnp.zeros_like(qga)
            kga[...] = jnp.zeros_like(kga)

        paced(e, 2, units, 6, run_unit)

        @pl.when(e == 8)
        def _():
            kv_two(batch - 1)
        paced(e, 8, batch * tiles, 3, run_fold)

        @pl.when(e == 10)
        def _():
            each(0, 2 * nz, settle)
            each(0, nz, lambda k: [swap(k, dr, kk).start() for dr in both for kk in both])

        @pl.when(e == 11)
        def _():
            for c in ld2:
                c.wait()
            total(sq, qs.at[1, 0])
            total(skv, qs.at[1, 1])
            each(0, nz, gather_h)
        paced(e, 11, events, 2, hblock)

        @pl.when(e == 12)
        def _():
            for j in (events - 2, events - 1):
                hstore(j).wait()
            first_fetch(1)

    each(0, events, step_c)

    def gblk(j):
        return qr.at[:, span(lax.rem(j, 2) * bw, bw)]

    def hblk(j):
        return gd.at[:, span(lax.rem(j, 2) * bw, bw)]

    def swo(j):
        return d_rows.at[pl.ds(0, qn), span(lax.rem(j, 2) * bw, bw)]

    def swq(j):
        return d_rows.at[pl.ds(pl.multiple_of(qn + lax.rem(j, 2) * bw, bw), bw), pl.ds(0, qn)]

    def g_load(j):
        return pltpu.make_async_copy(gy_out.at[:, span(j * bw, bw)], gblk(j), gls.at[lax.rem(j, 2)])

    def h_load(j):
        return pltpu.make_async_copy(hid.at[:, span(j * bw, bw)], hblk(j), hls.at[lax.rem(j, 2)])

    def wo_store(j):
        return pltpu.make_async_copy(swo(j), gwo_hbm.at[:, span(j * bw, bw)], swos.at[lax.rem(j, 2)])

    def wq_store(j):
        return pltpu.make_async_copy(swq(j), gq_hbm.at[span(j * bw, bw)], swqs.at[lax.rem(j, 2)])

    def block(j):
        g_load(j).wait()
        h_load(j).wait()

        @pl.when(j + 1 < events)
        def _():
            g_load(j + 1).start()
            h_load(j + 1).start()

        @pl.when(j >= 2)
        def _():
            wo_store(j - 2).wait()
            wq_store(j - 2).wait()
        cols = span(j * bw, bw)
        swo(j)[...] = dotf(o_own[...], gblk(j)[...], TN)
        ge_v[:, cols] = dotf(hotm[...], gblk(j)[...])
        wo_store(j).start()
        swq(j)[...] = dotf(hblk(j)[...], qt[...], TN)
        gkv_v[:, cols] = dotf(kvrow[...], hblk(j)[...], TN)[:2 * kn]
        wq_store(j).start()

    def final_h(dr, sub, gh):
        rows = span((2 * dr + sub) * sub_rows, sub_rows)
        x = gown[rows, :].astype(F32)
        r = lax.rsqrt(jnp.mean(x * x, axis=-1, keepdims=True) + EPS)
        ge_v[rows, :] += rms_pull(x, gh * gain[...], r)

    outs = [pltpu.make_async_copy(s, t, out_sem.at[i]) for i, (s, t) in enumerate((
        (y_v, y_hbm), (gkv_v.at[pl.ds(0, kn)], gk_hbm), (gkv_v.at[pl.ds(kn, kn)], gv_hbm)))]

    def ge_store(dr, sub):
        rows = pl.ds((2 * dr + sub) * sub_rows, sub_rows)
        return pltpu.make_async_copy(ge_v.at[rows], ge_hbm.at[rows], out_sem.at[3])

    g_load(0).start()
    h_load(0).start()
    outs[0].start()
    work_d = events - 3

    wide = gn_out.shape[1]
    gtop = d // wide
    mrow = gtop // 2

    def to_sib(t):
        if t:
            return rdma(gfin.at[core], gfin.at[core], gs.at[4], gs.at[5], sib)
        return rdma(gmine.at[1 - core], gsib, gs.at[0], gs.at[1], sib)

    def to_col(k):
        return rdma(gcol.at[z], gcol.at[z], gs.at[2], gs.at[3], 2 * lax.rem(z + k, nz) + core)

    def step_d(e):
        @pl.when(e >= 2)
        def _():
            serve(1, e, final_h)

        @pl.when(e == 0)
        def _():
            for k in both:
                for c in item(k):
                    c.start()

        paced(e, 2, events, 4, lambda j: hblock(j + events))

        @pl.when(e == 5)
        def _():
            for j in (events - 2, events - 1):
                hstore(j + events).wait()
        paced(e, 2, events, 8, gain_part)
        paced(e, 5, events, work_d - 5, block)

        @pl.when(e == 10)
        def _():
            whole = jnp.sum(gn[...], axis=0, keepdims=True)
            for k, extra in ((0, qga), (1, kga)):
                for j in range(mrow):
                    c0 = (k * mrow + j) * wide
                    gmine[k, j:j + 1, :] = whole[:, c0:c0 + wide].astype(BF)
                gmine[k, mrow:mrow + 1, :] = extra[...].astype(BF)
            to_sib(0).start()

        @pl.when(e == 11)
        def _():
            total(gsib, gs.at[1])
            gcol[z] = (gmine[core].astype(F32) + gsib[...].astype(F32)).astype(BF)
            for k in range(1, nz):
                to_col(k).start()

        @pl.when(e == 13)
        def _():
            total(gcol.at[pl.ds(0, nz - 1)], gs.at[3])
            gfin[core] = sum(gcol[k].astype(F32) for k in range(nz))
            to_sib(1).start()

        @pl.when(e == events - 3)
        def _():
            outs[1].start()
            outs[2].start()

        @pl.when(e == events - 2)
        def _():
            for dr in both:
                ge_store(dr, 0).start()

    each(0, events, step_d)

    for dr in both:
        ge_store(dr, 1).start()
    for ph in both:
        for k in range(4):
            arrived(rs.at[ph, k])

    total(gy_out.at[pl.ds(0, 2 * (events - 4) * pos)], b_s.at[1])
    total(gy_out.at[pl.ds(0, 2 * (events - 2) * pos)], b_s.at[3])
    to_far.wait_send()
    relay.wait_send()
    total(wpair.at[pl.ds(2 * qn, 2 * kn)], w_s.at[2])
    total(o_sib, o_s.at[0])
    total(pk.at[pl.ds(0, batch // 2)], p1s.at[0])
    total(fk, p2s.at[0])
    total(sq, qs.at[0, 0])
    total(skv, qs.at[0, 1])
    total(gfin.at[0], gs.at[5])
    gn_out[0:mrow, :] = gfin[0, 0:mrow, :]
    gn_out[mrow:, :] = gfin[1, 0:mrow, :]
    gqg_out[...] = gfin[0, mrow:mrow + 1, :]
    gkg_out[...] = gfin[1, mrow:mrow + 1, :]
    total(gsib, gs.at[0])
    total(gcol.at[pl.ds(0, nz - 1)], gs.at[2])
    total(gfin.at[0], gs.at[4])
    for j in (events - 2, events - 1):
        wo_store(j).wait()
        wq_store(j).wait()
    total(ge_v, out_sem.at[3])
    for c in outs:
        c.wait()


def step_kernel(nz, embed, gy, wq, wk_t, wv_t, wo, gain, qg, kg, cos, sin_s, tok_seq):
    vrows, d = embed.shape
    vocab = vrows * 2 * nz
    qn, kn = wq.shape[1], wk_t.shape[0]
    hd = qg.shape[1]
    batch, seq = tok_seq.shape
    toks = batch * seq
    ev = 2 * nz
    sr, hb, vh = vrows // 4, seq // 2, vocab // 2
    mr = (d // hd // 2 + 1 + 15) // 16 * 16
    dma = pltpu.SemaphoreType.DMA
    v = pltpu.VMEM

    def arr(dt, *shape):
        return jax.ShapeDtypeStruct(shape, dt)

    outs = (arr(BF, vrows, d), arr(F32, vrows, d), arr(F32, d, qn), arr(F32, kn, d), arr(F32, kn, d), arr(F32, qn, d), arr(F32, d // hd, hd), arr(F32, 1, hd), arr(F32, 1, hd), arr(BF, vh, d),
            arr(BF, vocab, d), arr(BF, toks, d), arr(BF, qn, d), arr(BF, qn, d), arr(F32, vh, d), arr(F32, vh, d))
    return pl.pallas_call(
        functools.partial(body, nz),
        name='step_kernel',
        out_shape=outs,
        in_specs=[ANY] * 6 + [VM] * 6,
        out_specs=(ANY,) * 6 + (VM,) * 3 + (ANY,) * 7,
        scratch_shapes=[v((vocab, d), BF), v((2 * qn + 4 * kn, d), BF), v((max(d, 2 * toks), qn), BF), v((vocab, qn), BF), v((toks, qn), BF), v((vh, qn), BF), v((vh, qn), BF),
                        v((toks, 2 * hd), BF), v((toks, hd), BF), v((2, toks // 2, 4 * kn), BF), v((2, toks // 2, 4 * kn), BF), v((vocab, 4 * kn), BF), v((vh, 4 * kn), BF), v((vh, 4 * kn), BF),
                        v((vocab, qn + 4 * kn), F32), v((4, 2, sr, d), F32), v((2, vrows, d), BF), v((vrows, d), BF), v((vrows, toks), BF),
                        v((seq, hd), F32), v((seq, hd), F32), v((batch, 4, hb, 4 * kn), BF), v((batch, 2, hb, 4 * kn), BF), v((batch, hb, 4 * kn), BF), v((batch, hb, 4 * kn), F32),
                        v((batch, hb, 4 * kn), BF), v((batch, seq, 4 * kn), BF), v((8, d), F32), v((1, hd), F32), v((1, hd), F32), v((2, mr, hd), BF), v((mr, hd), BF), v((nz, mr, hd), BF), v((2, mr, hd), F32), v((vrows, d), BF), v((vrows, d), F32), v((2 * kn, d), F32),
                        dma((12,)), dma((2,)), dma((1,)), dma((ev,)), dma((ev,)), dma((2,)), dma((4,)), dma((2,)), dma((2,)), dma((2, 2)), dma((1,)), dma((4,)), dma((2,)),
                        dma((2,)), dma((2, 2)), dma((2, 4)), dma((1,)), dma((batch,)), dma((1,)), dma((batch,)), dma((2, 2)),
                        dma((2,)), dma((2,)), dma((2,)), dma((2,)), dma((6,)), dma((4,)), dma((3,))],
        compiler_params=pltpu.CompilerParams(collective_id=0, has_side_effects=True, vmem_limit_bytes=67043328),
        cost_estimate=pl.CostEstimate(flops=2 * vocab * d * 8 * qn, bytes_accessed=20 * vocab * d, transcendentals=0),
    )(embed, gy, wq, wk_t, wv_t, wo, gain, qg, kg, cos, sin_s, tok_seq)


def emit_body(cuts, *refs):
    n = len(cuts)
    src, dst = refs[:n], refs[n:2 * n]
    bufs, s_in, s_out = refs[2 * n:-2], refs[-2], refs[-1]
    ins, outs = [], []
    for i, c in enumerate(cuts):
        step = src[i].shape[0] // c
        for j in range(c):
            b = bufs[i].at[pl.ds(j * step, step)]
            ins.append(pltpu.make_async_copy(src[i].at[pl.ds(j * step, step)], b, s_in.at[len(ins)]))
            outs.append(pltpu.make_async_copy(b, dst[i].at[pl.ds(j * step, step)], s_out.at[len(outs)]))
    for c in ins:
        c.start()
    for a, b in zip(ins, outs):
        a.wait()
        b.start()
    for b in outs:
        b.wait()


def emit(*arrays):
    size = 1 << 20
    cuts = tuple(max(1, a.size * a.dtype.itemsize // size) for a in arrays)
    return pl.pallas_call(
        functools.partial(emit_body, cuts),
        name='emit',
        out_shape=tuple(jax.ShapeDtypeStruct(a.shape, a.dtype) for a in arrays),
        in_specs=[ANY] * len(arrays),
        out_specs=(ANY,) * len(arrays),
        scratch_shapes=[pltpu.VMEM(a.shape, a.dtype) for a in arrays] + [pltpu.SemaphoreType.DMA((sum(cuts),))] * 2,
        compiler_params=pltpu.CompilerParams(vmem_limit_bytes=60 * 1024 * 1024),
        cost_estimate=pl.CostEstimate(flops=0, bytes_accessed=2 * sum(a.size * a.dtype.itemsize for a in arrays), transcendentals=0),
    )(*arrays)


def rope_consts(seq, hd):
    inv = np.float32(ROPE_BASE) ** (np.float32(-2.0) * np.arange(hd // 2, dtype=np.float32) / np.float32(hd))
    ang = np.arange(seq, dtype=np.float32)[:, None] * inv.astype(np.float32)[None, :]
    ang = np.concatenate([ang, ang], axis=-1)
    sign = np.where(np.arange(hd) < hd // 2, -1.0, 1.0).astype(np.float32)
    return np.cos(ang).astype(np.float32), (np.sin(ang) * sign).astype(np.float32)


def solution(mesh):
    tp = mesh.shape['tp']
    nz = tp // 2

    def local_step(tok_ids, embed_loc, norm_gain, q_gain, k_gain, wq, wk, wv, wo, gy_loc):
        d_model = embed_loc.shape[1]
        batch, seq = tok_ids.shape
        seq_dev = seq // tp
        hd = q_gain.shape[0]
        cos_c, sin_c = (jnp.asarray(t) for t in rope_consts(seq, hd))
        r = step_kernel(nz, embed_loc, gy_loc.reshape(batch * seq_dev, d_model), wq, wk.T, wv.T, wo, norm_gain[None, :], q_gain[None, :], k_gain[None, :], cos_c, sin_c, tok_ids)
        y, g_embed, g_wq, g_wk, g_wv, g_wo, g_n, g_q, g_k = emit(*r[:9])
        return (y.reshape(batch, seq_dev, d_model), g_embed, g_n.reshape(d_model), g_q.reshape(hd), g_k.reshape(hd), g_wq, g_wk.T, g_wv.T, g_wo)

    in_specs = (P('dp', None), P('tp', None), P(), P(), P(), P(None, 'tp'), P(None, 'tp'), P(None, 'tp'), P('tp', None), P('dp', 'tp', None))
    out_specs = (P('dp', 'tp', None), P(('dp', 'tp'), None), P('dp'), P('dp'), P('dp'), P('dp', 'tp'), P('dp', 'tp'), P('dp', 'tp'), P(('dp', 'tp'), None))
    return jax.shard_map(local_step, mesh=mesh, in_specs=in_specs, out_specs=out_specs, check_vma=False)
```

profile of v0, /device:TPU:21, one launch (start us, length us, event | category | flops | bytes accessed | tf_op | source)
XLA Modules:
  0.0 356.0 jit_solution(8275136609260819812)
XLA Ops:
  0.6 340.3 %step_kernel.1 = (bf16[128,4096]{1,0:T(8,128)(2,1)}, f32[128,4096]{1,0:T(8,128)}, f32[4096,512]{1,0:T(8,128)}, f32[32,4096]{1,0:T(8,128)}, f32[32,4096]{1,0:T(8,...) custom-call(bf16[128,4096]{1,0:T(8,128)(2,1)} %embed.1, ...), custom_call_target="tpu_custom_call" | custom-call | flops 68719476736 | bytes 167772160 | tf_op jit(solution)/shard_map/step_kernel/pallas_call | solution.py:910
  341.0 14.8 %emit.1 = (bf16[128,4096]{1,0:T(8,128)(2,1)}, f32[128,4096]{1,0:T(8,128)}, f32[4096,512]{1,0:T(8,128)}, f32[32,4096]{1,0:T(8,128)}, f32[32,4096]{1,0:T(8,128)}, ...) custom-call(bf16[128,4096]{1,0:T(8,128)(2,1)} %get-tuple-element.27.refs_0_, ...), custom_call_target="tpu_custom_call" | custom-call | bytes 41977856 | tf_op jit(solution)/shard_map/emit/pallas_call | solution.py:952
where the time goes:
time: 356 us
  Pallas kernels  355 us (100%)
    pallas_call x1, Pallas kernels, step_kernel(): pl.pallas_call(functools.partial(body, nz), name='step_kernel', out_shape...  340 us
    pallas_call x1, Pallas kernels, emit(): pl.pallas_call(functools.partial(emit_body, cuts), name='emit', out_shape...  14.8 us

commit v1 on v0

v1 whole, which is shorter than its diff:
```python
import functools
import jax
import jax.numpy as jnp
import numpy as np
from jax import lax
from jax.experimental import pallas as pl
from jax.experimental.pallas import tpu as pltpu
from jax.sharding import PartitionSpec as P

BF = jnp.bfloat16
F32 = jnp.float32
EPS = 1.0e-6
ROPE_BASE = 1.0e6
NEG_BIG = -1.0e30
LOG2E = 1.4426950408889634
MESH = pl.DeviceIdType.MESH
ANY = pl.BlockSpec(memory_space=pl.ANY)
VM = pl.BlockSpec(memory_space=pltpu.VMEM)
NT = (((1,), (1,)), ((), ()))
NN = (((1,), (0,)), ((), ()))
TN = (((0,), (0,)), ((), ()))


def dotf(a, b, dims=NN):
    return lax.dot_general(a, b, dims, preferred_element_type=F32)


def rdma(src, dst, ssem, rsem, dev):
    return pltpu.make_async_remote_copy(src_ref=src, dst_ref=dst, send_sem=ssem, recv_sem=rsem, device_id={'tp': dev}, device_id_type=MESH)


def span(start, size):
    return pl.ds(pl.multiple_of(start, size), size)


def each(lo, hi, f):
    def go(j, _):
        f(j)
        return 0
    lax.fori_loop(lo, hi, go, 0)


def total(ref, sem):
    pltpu.make_async_copy(ref, ref, sem).wait()


def odd(e):
    return lax.rem(e, 2)


def piece(dr, e):
    return 2 * dr + lax.rem(e, 2)


def lead(n):
    return pl.ds(0, n)


def half(n):
    return n // 2


def row_sum(t):
    return jnp.sum(t, axis=-1, keepdims=True)


def row_mean(t):
    return jnp.mean(t, axis=-1, keepdims=True)


def row_ids(shape):
    return lax.broadcasted_iota(jnp.int32, shape, 0)


def col_ids(shape):
    return lax.broadcasted_iota(jnp.int32, shape, 1)


def chosen(mask):
    return jnp.where(mask, 1.0, 0.0).astype(BF)


def rms_f32(x, gain):
    return x * lax.rsqrt(row_mean(x * x) + EPS) * gain


def rms_pull(x, dxr, r):
    return r * dxr - x * (r * r * r * row_mean(x * dxr))


def causal_blocks(q, keys, i, blk):
    r_i = row_ids((blk, blk))
    c_i = col_ids((blk, blk))
    s = [dotf(q, keys[j * blk:(j + 1) * blk], NT) for j in range(i + 1)]
    s[i] = jnp.where(r_i >= c_i, s[i], NEG_BIG)
    top = functools.reduce(jnp.maximum, [jnp.max(t, axis=-1, keepdims=True) for t in s])
    c = q.shape[-1] ** -0.5 * LOG2E
    e = [jnp.exp2((t - top) * c) for t in s]
    inv = 1.0 / sum(row_sum(t) for t in e)
    return [t * inv for t in e]


def body(nz, embed, gy, wq, wk_t, wv_t, wo, gain, qg, kg, cos, sin_s, tok_seq,
         y_hbm, ge_hbm, gq_hbm, gk_hbm, gv_hbm, gwo_hbm, gn_out, gqg_out, gkg_out, erows, hid, gy_out, wqt_out, wqts_out, py_out, ph_out,
         table, wpair, wq_v, qt, o_own, o_sib, sq, kv_tok, k_rot, kvacc, farkv, kvrow, skv, kvc, d_rows, pbuf, hbuf, gown, hotm,
         dk_acc, dv_acc, pk, rk1, fk, hk, rk2, kvt, gn, qga, kga, gmine, gsib, gcol, gfin, y_v, ge_v, gkv_v,
         in_sem, h_sem, g_sem, r_sem, s_sem, a_s, b_s, xs, xr, wq_s, wq_r, w_s, o_s, pt_sem, pl_sem, rs, p1s, p1r, p2s, p2r, qs, gls, hls, swos, swqs, gs, out_sem, e_sem):
    rank = lax.axis_index('tp')
    z, core = half(rank), odd(rank)
    right = 2 * lax.rem(z + 1, nz) + core
    left = 2 * lax.rem(z + nz - 1, nz) + core
    sib = rank + 1 - 2 * core
    par = odd(z)
    far = rank + 2 - 4 * par
    vrows, d = embed.shape
    kn = wk_t.shape[0]
    sub_rows = vrows // 4
    events = 2 * nz
    vocab = vrows * events
    last, final_e = events - 2, events - 1
    kw, kh, sr2 = 4 * kn, 2 * kn, vrows // 2
    vhalf = half(vocab)
    batch, seq = tok_seq.shape
    toks = batch * seq
    qn = wq.shape[1]
    q2 = 2 * qn
    hd = qg.shape[1]
    heads = qn // hd
    pos = seq // events
    blk = half(seq)
    bw = d // events
    scale = hd ** -0.5
    units = batch * heads
    parts = 8
    wo_p, wq_p = qn // parts, d // parts
    both = (0, 1)
    places = [(dr, c) for dr in both for c in both]
    qr = wq_v.at[lead(toks)]
    gd = wq_v.at[pl.ds(toks, toks)]
    w_q = wq_v.at[lead(d)]

    ld = [pltpu.make_async_copy(s, t, in_sem.at[i]) for i, (s, t) in enumerate((
        (embed, table.at[span(rank * vrows, vrows)]), (gy, gown), (wq, w_q), (wo, wpair.at[lead(qn)]),
        (wk_t, wpair.at[pl.ds(q2, kn)]), (wv_t, wpair.at[pl.ds(q2 + kn, kn)])))]
    ld2 = [pltpu.make_async_copy(s, t, in_sem.at[i]) for i, (s, t) in enumerate((
        (wqt_out, wpair.at[lead(qn)]), (wqts_out, wpair.at[pl.ds(qn, qn)]), (embed, gown)))]
    ld[0].start()
    barrier = pltpu.get_barrier_semaphore()
    for dev in (right, left, sib):
        pl.semaphore_signal(barrier, inc=1, device_id={'tp': dev}, device_id_type=MESH)
    pl.semaphore_wait(barrier, 3)
    ld[0].wait()

    def nbr(dr):
        return right if dr == 0 else left

    def arrived(sem):
        total(table.at[lead(sr2)], sem)

    def zd_of(dr, e):
        s = half(e)
        return lax.rem(z + (nz - s if dr == 0 else s), nz)

    def row_of(dr, e, c):
        return pl.multiple_of(vrows * (2 * zd_of(dr, e) + c) + sub_rows * (piece(dr, e)), sub_rows)

    def ring(dr, e, recv_e):
        a = table.at[pl.ds(row_of(dr, e, core), sub_rows)]
        return rdma(a, a, a_s.at[0], r_sem.at[recv_e], nbr(dr))

    def side(dr, e):
        a = table.at[pl.ds(row_of(dr, e, core), sub_rows)]
        return rdma(a, a, a_s.at[1], s_sem.at[e], sib)

    def e_keep(dr, e):
        dst = pl.multiple_of(vrows * lax.rem(half(e) + nz - 1, nz) + sub_rows * (piece(dr, e)), sub_rows)
        return pltpu.make_async_copy(table.at[pl.ds(row_of(dr, e, core), sub_rows)], erows.at[pl.ds(dst, sub_rows)], e_sem.at[0])

    def h_copy(slot, i, row):
        return pltpu.make_async_copy(hbuf.at[slot, pl.ds(i * sub_rows, sub_rows)], hid.at[pl.ds(row, sub_rows)], h_sem.at[slot])

    def g_row(dr, e, c):
        return pl.multiple_of(seq * (piece(dr, e)) + pos * (2 * zd_of(dr, e) + c), pos)

    def g_piece(dr, e, c):
        return gy_out.at[pl.ds(g_row(dr, e, c), pos)]

    def g_own(dr, e):
        return gown.at[span(pos * (piece(dr, e)), pos)]

    def g_ring(dr, e, recv_e, first):
        a = g_piece(dr, e, core)
        return rdma(g_own(dr, e) if first else a, a, b_s.at[0 if first else 1], r_sem.at[recv_e], nbr(dr))

    def g_side(dr, e, first):
        a = g_piece(dr, e, core)
        return rdma(g_own(dr, e) if first else a, a, b_s.at[2 if first else 3], s_sem.at[e], sib)

    def g_home(dr, e):
        return pltpu.make_async_copy(g_own(dr, e), g_piece(dr, e, core), in_sem.at[8 + 2 * dr + e])

    def g_fetch(slot, i, dr, c, e):
        return pltpu.make_async_copy(g_piece(dr, e, c), hbuf.at[slot, pl.ds(i * pos, pos)], g_sem.at[0])

    def wo_push(k):
        return rdma(wpair.at[span(k * wo_p, wo_p)], wpair.at[pl.ds(pl.multiple_of(qn + k * wo_p, wo_p), wo_p)], w_s.at[0], w_s.at[1], sib)

    def tb(k):
        return o_own.at[span(odd(k) * qn, qn), lead(wq_p)]

    def wq_push(k):
        return rdma(tb(k), wqts_out.at[:, span(k * wq_p, wq_p)], wq_s.at[0, odd(k)], wq_r.at[0], sib)

    def wq_home(k):
        return pltpu.make_async_copy(tb(k), wqt_out.at[:, span(k * wq_p, wq_p)], wq_s.at[1, odd(k)])

    def wk_push(k):
        return rdma((wk_t, wv_t)[k], wpair.at[pl.ds(q2 + (2 + k) * kn, kn)], w_s.at[2], w_s.at[3], sib)

    def o_push(b, k):
        src = pl.multiple_of(b * seq + pos * (2 * k + 1 - core), pos)
        dst = pl.multiple_of(vrows * k + pos * b, pos)
        return rdma(o_own.at[pl.ds(src, pos)], o_sib.at[pl.ds(dst, pos)], o_s.at[0], o_s.at[1], sib)

    def project(e):
        slot = odd(e)

        @pl.when(e >= 2)
        def _():
            total(hbuf.at[slot], h_sem.at[slot])

        rows = [row_of(dr, e, c) for dr, c in places]
        for i, row in enumerate(rows):
            x = table[pl.ds(row, sub_rows), :].astype(F32)
            ids = row + row_ids((sub_rows, seq))
            hit = jnp.zeros((sub_rows, seq), F32)
            for b in range(batch):
                hit = jnp.maximum(hit, jnp.where(tok_seq[b:b + 1, :] == ids, 1.0, 0.0))
            used = jnp.max(hit, axis=1, keepdims=True)
            h = jnp.where(used > 0.5, rms_f32(x, gain[:]), 0.0)
            hbuf[slot, pl.ds(i * sub_rows, sub_rows), :] = h.astype(BF)
            h_copy(slot, i, row).start()
        hb = hbuf[slot]
        qkv = jnp.concatenate([dotf(hb, w_q[:]).astype(BF), dotf(hb, wpair[q2:q2 + kw, :], NT).astype(BF)], axis=1)
        lane = col_ids((1, vrows))
        rowid = jnp.zeros((1, vrows), jnp.int32)
        for i, row in enumerate(rows):
            rowid = jnp.where(lane // sub_rows == i, row + lane - i * sub_rows, rowid)
        rowid = rowid.astype(F32)
        for b in range(batch):
            sl = slice(b * seq, (b + 1) * seq)
            hot = chosen(d_rows[sl, :vrows] == rowid)
            got = dotf(hot, qkv)
            qt[sl, :] = (qt[sl, :].astype(F32) + got[:, :qn]).astype(BF)
            at = slice((b % 2) * seq, (b % 2 + 1) * seq)
            kvacc[b // 2, at, :] = (kvacc[b // 2, at, :].astype(F32) + got[:, qn:]).astype(BF)

    def step_a(e):
        @pl.when((e >= 2) & (e < events))
        def _():
            arrived(r_sem.at[e])

        @pl.when(e < last)
        def _():
            for dr in both:
                ring(dr, e, e + 2).start()

        @pl.when(e < events)
        def _():
            for dr in both:
                side(dr, e).start()
                e_keep(dr, e).start()

        @pl.when(e == 0)
        def _():
            for c in ld[1:]:
                c.start()
            for k in both:
                wk_push(k).start()
            for b in range(batch):
                wide = jnp.broadcast_to(tok_seq[b:b + 1, :].astype(F32), (vrows, seq))
                d_rows[b * seq:(b + 1) * seq, :vrows] = wide.T
            qt[:] = jnp.zeros_like(qt)
            kvacc[:] = jnp.zeros_like(kvacc)

        @pl.when(e == 1)
        def _():
            for c in ld[1:]:
                c.wait()
            total(wpair.at[pl.ds(q2, kh)], w_s.at[3])
            for dr in both:
                for k in both:
                    g_home(dr, k).start()

        @pl.when((e >= last) & (e < events))
        def _():
            for dr in both:
                g_ring(dr, e - events + 2, e - events + 4, True).start()

        @pl.when((e >= 2) & (e < 4 + parts))
        def _():
            @pl.when(e >= 4)
            def _():
                wq_push(e - 4).wait_send()
                wq_home(e - 4).wait()

            @pl.when(e < 2 + parts)
            def _():
                k = e - 2
                block = wq_v[span(k * wq_p, wq_p), :]
                tb(k)[:] = block.astype(F32).T.astype(BF)
                wo_push(k).start()
                wq_push(k).start()
                wq_home(k).start()

        @pl.when(e >= 1)
        def _():
            arrived(s_sem.at[e - 1])
            project(e - 1)

    each(0, events + 1, step_a)

    to_far = rdma(kvacc.at[core], farkv.at[core], xs.at[0], xr.at[0], far)
    relay = rdma(farkv.at[core], farkv.at[core], xs.at[1], xr.at[1], sib)
    at_i = col_ids((pos, seq)) - pos * rank
    own_i = row_ids((pos, seq))
    col = jnp.concatenate([jnp.sum(jnp.where(at_i == own_i, tok_seq[b:b + 1, :].astype(F32), 0.0), axis=1, keepdims=True) for b in range(batch)], axis=0).astype(jnp.int32)
    lanes = col_ids((vrows, vrows))
    hot_mine = jnp.concatenate([chosen(col == lanes + j * vrows) for j in range(vocab // vrows)], axis=1)
    to_far.start()
    for dr in both:
        for k in both:
            g_side(dr, k, True).start()
            g_home(dr, k).wait()
    cw = min(512, d)

    def own_rows(j):
        y_v[:, span(j * cw, cw)] = dotf(hot_mine, table[:, span(j * cw, cw)]).astype(BF)

    each(0, d // cw, own_rows)
    for b in range(batch):
        ids = rank * vrows + row_ids((vrows, seq))
        hotm[:, b * seq:(b + 1) * seq] = chosen(ids == tok_seq[b:b + 1, :])

    def place(p, first):
        l_i = row_ids((kw, 2 * hd))
        m_i = col_ids((kw, 2 * hd))
        upper = jnp.where(l_i >= kh, 1, 0)
        owner = jnp.where(upper == 1, 1 - first, first)
        l_i = l_i - kh * upper
        base = kn * (2 * p + owner)
        want = jnp.where(l_i < kn, base + l_i, hd + base + l_i - kn)
        return chosen(m_i == want)

    def rope(raw, g):
        n = rms_f32(raw.astype(F32), g)
        return (n * cos[:] + pltpu.roll(n, half(hd), 1) * sin_s[:]).astype(BF)

    def attend(u):
        base = (u // heads) * seq
        rows = span(base, seq)
        cols = span(lax.rem(u, heads) * hd, hd)
        q = rope(qt[rows, cols], qg[:])
        qr[rows, cols] = q
        kr = k_rot[rows, :]
        v = kv_tok[rows, hd:]
        for i in both:
            p = causal_blocks(q[i * blk:(i + 1) * blk], kr, i, blk)
            o = sum(dotf(t.astype(BF), v[j * blk:(j + 1) * blk]) for j, t in enumerate(p))
            o_own[pl.ds(pl.multiple_of(base + i * blk, blk), blk), cols] = o.astype(BF)

    def grad_attend(e):
        total(hbuf, g_sem.at[0])
        r = dotf(hbuf[:].reshape(2 * vrows, d), wpair[:qn, :], NT).astype(BF)
        for k in both:
            for i, (dr, c) in enumerate(places):
                n = (4 * k + i) * pos
                gd[pl.ds(g_row(dr, e + k, c), pos), :] = r[n:n + pos]

    def pstage(j):
        return d_rows.at[span(odd(j) * vhalf, vhalf), lead(bw)]

    def pstore(dst, j):
        return pltpu.make_async_copy(pstage(j), dst.at[:, span(j * bw, bw)], pt_sem.at[odd(j)])

    def pblock(dst, j, pairs):
        @pl.when(j >= 2)
        def _():
            pstore(dst, j - 2).wait()
        cols = span(j * bw, bw)
        acc = None
        for a, lo, n in pairs:
            t = dotf(a[:], wpair[lo:lo + n, cols])
            acc = t if acc is None else acc + t
        pstage(j)[:] = acc
        pstore(dst, j).start()

    y_pairs = [(sq, 0, qn), (o_sib, qn, qn)]

    def pslot(ph, e, dr):
        return pbuf.at[2 * ph + odd(e), dr]

    def pfetch(ph, e, dr):
        s = half(e)
        step = s if ph else lax.rem(z + (final_e - s if dr == 0 else 1 + s), nz)
        row = pl.multiple_of(vrows * step + sub_rows * (piece(dr, e)), sub_rows)
        return pltpu.make_async_copy((py_out, ph_out)[ph].at[pl.ds(row, sub_rows)], pslot(ph, e, dr), pl_sem.at[ph, odd(e)])

    def item(i):
        row = vrows * (half(i))
        cps = []
        for dr in both:
            at = pl.ds(pl.multiple_of(row + sub_rows * (2 * dr + odd(i)), sub_rows), sub_rows)
            cps.append(pltpu.make_async_copy(ph_out.at[at], pbuf.at[odd(i), dr], pl_sem.at[0, odd(i)]))
            cps.append(pltpu.make_async_copy(erows.at[at], hbuf.at[odd(i), pl.ds(dr * sub_rows, sub_rows)], e_sem.at[1 + odd(i)]))
        return cps

    def gain_part(i):
        total(pbuf.at[odd(i)], pl_sem.at[0, odd(i)])
        total(hbuf.at[odd(i), lead(sr2)], e_sem.at[1 + odd(i)])
        for dr in both:
            x = hbuf[odd(i), dr * sub_rows:(dr + 1) * sub_rows, :].astype(F32)
            t = pbuf[odd(i), dr] * (x * lax.rsqrt(row_mean(x * x) + EPS))
            gn[:] += sum(t[k:k + 8] for k in range(0, sub_rows, 8))

        @pl.when(i + 2 < events)
        def _():
            for c in item(i + 2):
                c.start()

    def fetched(ph, e):
        total(pbuf.at[2 * ph + odd(e)], pl_sem.at[ph, odd(e)])

    def rslot(dr, e):
        return table.at[span((dr * (last) + e) * sub_rows, sub_rows)]

    def sslot(ph, dr, e):
        k = 2 * (last) + 8 * ph + 4 * odd(half(e)) + piece(dr, e)
        return table.at[span(k * sub_rows, sub_rows)]

    def send(ph, dr, e):
        return rdma(sslot(ph, dr, e), rslot(dr, e), rs.at[ph, lax.rem(e, 4)], r_sem.at[e + 2], nbr(dr))

    def first_fetch(ph):
        for e in both:
            for dr in both:
                pfetch(ph, e, dr).start()

    def first_sends(ph):
        for e in both:
            fetched(ph, e)
            for dr in both:
                sslot(ph, dr, e)[:] = pslot(ph, e, dr)[:].astype(BF)
        for e in both:
            for dr in both:
                send(ph, dr, e).start()
                pfetch(ph, e + 2, dr).start()

    def serve(ph, e, final):
        arrived(r_sem.at[e])
        fetched(ph, e)

        @pl.when(e < last)
        def _():
            @pl.when(e >= 4)
            def _():
                arrived(rs.at[ph, lax.rem(e, 4)])
            for dr in both:
                sslot(ph, dr, e)[:] = (pslot(ph, e, dr)[:] + rslot(dr, e - 2)[:].astype(F32)).astype(BF)
            for dr in both:
                send(ph, dr, e).start()
                pfetch(ph, e + 2, dr).start()

        @pl.when(e >= last)
        def _():
            for dr in both:
                final(dr, odd(e), pslot(ph, e, dr)[:] + rslot(dr, e - 2)[:].astype(F32))

    slots = 9

    def gather_o(k):
        for b in range(batch):
            src = pl.multiple_of(b * seq + pos * (2 * k + core), pos)
            sq[pl.ds(pl.multiple_of(vrows * k + pos * b, pos), pos), :] = o_own[pl.ds(src, pos), :]

    def upto(e, n, over):
        return jnp.minimum((e * n) // over, n)

    def step_b(e):
        @pl.when(e == last)
        def _():
            first_sends(0)

        @pl.when((e >= 2) & (e < events))
        def _():
            arrived(r_sem.at[e])

        @pl.when((e >= 2) & (e < last))
        def _():
            for dr in both:
                g_ring(dr, e, e + 2, False).start()

        @pl.when((e >= 2) & (e < events))
        def _():
            for dr in both:
                g_side(dr, e, False).start()

        @pl.when((e >= 1) & (e <= events))
        def _():
            arrived(s_sem.at[e - 1])

        @pl.when(e == 2)
        def _():
            to_far.wait_recv()
            relay.start()

        @pl.when(e == 3)
        def _():
            rdma(farkv.at[1 - core], farkv.at[1 - core], xs.at[1], xr.at[1], sib).wait_recv()
            for hf in both:
                kv_tok[hf * (half(toks)):(hf + 1) * (half(toks)), :] = (dotf(kvacc[hf], place(par, core)) + dotf(farkv[hf], place(1 - par, hf))).astype(BF)
            for b in range(batch):
                sl = slice(b * seq, (b + 1) * seq)
                k_rot[sl, :] = rope(kv_tok[sl, :hd], kg[:])

        @pl.when((e >= 2) & (odd(e) == 0))
        def _():
            for k in both:
                for i, (dr, c) in enumerate(places):
                    g_fetch(k, i, dr, c, e - 2 + k).start()

        def give(b):
            each(0, nz, lambda k: o_push(b, k).start())

        def seen(t):
            return jnp.minimum((jnp.maximum(t - 3, 0) * units) // (slots - 3), units)

        each(seen(e - 1) // heads, seen(e) // heads, give)
        each(seen(e), seen(e + 1), attend)

        @pl.when(e == 4)
        def _():
            total(table.at[lead(2 * (last) * sub_rows)], a_s.at[0])
            total(table.at[lead(2 * events * sub_rows)], a_s.at[1])
            total(erows, e_sem.at[0])

        @pl.when(e == slots + 1)
        def _():
            total(wpair.at[lead(qn)], w_s.at[1])
            total(o_sib, o_s.at[1])
            each(0, nz, gather_o)

        @pl.when((e > slots) & (e <= slots + 4))
        def _():
            each(4 * (e - slots - 1), 4 * (e - slots), lambda j: pblock(py_out, j, y_pairs))

        @pl.when(e == slots + 4)
        def _():
            for j in (last, final_e):
                pstore(py_out, j).wait()
            first_fetch(0)

        @pl.when((e >= 3) & (odd(e) == 1))
        def _():
            grad_attend(e - 3)

    for slot in both:
        total(hbuf.at[slot], h_sem.at[slot])
    each(0, events + 2, step_b)

    def pull(raw, dout, g):
        x = raw.astype(F32)
        r = lax.rsqrt(row_mean(x * x) + EPS)
        dn = dout * cos[:] + pltpu.roll(dout * sin_s[:], half(hd), 1)
        return rms_pull(x, dn * g, r).astype(BF), jnp.sum(dn * (x * r), axis=0, keepdims=True)

    def unit(u):
        b, h = u // heads, lax.rem(u, heads)
        rows = span(b * seq, seq)
        cols = span(h * hd, hd)

        @pl.when(h == 0)
        def _():
            dk_acc[:] = jnp.zeros_like(dk_acc)
            dv_acc[:] = jnp.zeros_like(dv_acc)
        q, g = qr[rows, cols], gd[rows, cols]
        kr, v = k_rot[rows, :], kv_tok[rows, hd:]
        dqs = []
        for i in both:
            qi, gi = q[i * blk:(i + 1) * blk], g[i * blk:(i + 1) * blk]
            p = causal_blocks(qi, kr, i, blk)
            dp = [dotf(gi, v[j * blk:(j + 1) * blk], NT) for j in range(i + 1)]
            tot = sum(row_sum(a * b) for a, b in zip(p, dp))
            dq = None
            for j in range(i + 1):
                at = slice(j * blk, (j + 1) * blk)
                dv_acc[at, :] += dotf(p[j].astype(BF), gi, TN)
                ds = (p[j] * (dp[j] - tot)).astype(BF)
                t = dotf(ds, kr[at])
                dq = t if dq is None else dq + t
                dk_acc[at, :] += dotf(ds, qi, TN)
            dqs.append(dq * scale)
        dq = jnp.concatenate(dqs, axis=0).astype(BF).astype(F32)
        dx, dg = pull(qt[rows, cols], dq, qg[:])
        gd[rows, cols] = dx
        qga[:] += dg

    def pick(r, up):
        m_i = row_ids((2 * hd, kw))
        l_i = col_ids((2 * hd, kw)) - kh * up
        is_k = (l_i >= 0) & (l_i < kn) & (m_i == l_i + kn * r)
        is_v = (l_i >= kn) & (l_i < kh) & (m_i == hd + kn * r + l_i - kn)
        return chosen(is_k | is_v)

    def to_side(b, p):
        return rdma(pk.at[b, 2 * p + 1 - core], rk1.at[b, p], p1s.at[0], p1r.at[b], sib)

    def to_far2(b):
        return rdma(fk.at[b], rk2.at[b], p2s.at[0], p2r.at[b], far)

    def kv_one(b):
        dk = (dk_acc[:] * scale).astype(BF).astype(F32)
        dx, dg = pull(kv_tok[span(b * seq, seq), :hd], dk, kg[:])
        kga[:] += dg
        gkv = jnp.concatenate([dx, dv_acc[:].astype(BF)], axis=1)
        for r in range(4):
            pk[b, r] = (dotf(gkv[:blk], pick(r, 0)) + dotf(gkv[blk:], pick(r, 1))).astype(BF)
        for p in both:
            to_side(b, p).start()

    def kv_two(b):
        total(rk1.at[b], p1r.at[b])
        fk[b] = (pk[b, 2 * (1 - par) + core].astype(F32) + rk1[b, 1 - par].astype(F32)).astype(BF)
        hk[b] = pk[b, 2 * par + core].astype(F32) + rk1[b, par].astype(F32)
        to_far2(b).start()

    def kv_three(b):
        to_far2(b).wait_recv()
        t = hk[b] + rk2[b].astype(F32)
        low = col_ids(t.shape) < kh
        kvt[b, :blk, :] = jnp.where(low, t, 0.0).astype(BF)
        kvt[b, blk:, :] = jnp.where(low, pltpu.roll(t, kh, 1), 0.0).astype(BF)

    def fold(b, tile):
        rows = span(tile * seq, seq)
        ids = tile * seq + row_ids((seq, seq))
        hot = chosen(ids == tok_seq[pl.ds(b, 1), :])
        d_rows[rows, :qn] += dotf(hot, gd[span(b * seq, seq), :])
        d_rows[rows, qn:] += dotf(hot, kvt[b])

    tiles = vocab // seq

    def run_unit(u):
        unit(u)

        @pl.when(lax.rem(u, heads) == heads - 1)
        def _():
            kv_one(u // heads)

        @pl.when((u >= heads) & (lax.rem(u, heads) == 1))
        def _():
            kv_two(u // heads - 1)

    def run_fold(f):
        b, tile = f // tiles, lax.rem(f, tiles)

        @pl.when(tile == 0)
        def _():
            kv_three(b)
        fold(b, tile)

    def share(e, first, n, over):
        return jnp.minimum((jnp.maximum(e - first, 0) * n) // over, n)

    def paced(e, first, n, over, f):
        each(share(e, first, n, over), share(e + 1, first, n, over), f)

    def settle(t):
        rows = span(t * vrows, vrows)
        qt[rows, :] = d_rows[rows, :qn].astype(BF)
        kvrow[rows, :] = d_rows[rows, qn:].astype(BF)

    def step_row(k, dr):
        return pl.multiple_of(vrows * lax.rem(z + nz - 1 - k if dr == 0 else k + nz - 1 - z, nz) + sr2 * dr, sr2)

    def swap(k, dr, kk):
        src = pl.multiple_of(vrows * (2 * k + 1 - core) + sr2 * dr, sr2)
        return rdma((qt, kvrow)[kk].at[pl.ds(src, sr2)], (sq, skv)[kk].at[pl.ds(step_row(k, dr), sr2)], qs.at[0, kk], qs.at[1, kk], sib)

    def gather_h(k):
        for dr in both:
            src = pl.multiple_of(vrows * (2 * k + core) + sr2 * dr, sr2)
            dst = pl.ds(step_row(k, dr), sr2)
            o_sib[dst, :] = qt[pl.ds(src, sr2), :]
            kvc[dst, :] = (kvrow[pl.ds(src, sr2), :].astype(F32) + pltpu.roll(skv[dst, :].astype(F32), kh, 1)).astype(BF)

    hrows = half(vhalf)

    def hstage(j):
        return d_rows.at[pl.ds(pl.multiple_of(vhalf + odd(j) * hrows, hrows), hrows), lead(bw)]

    def hstore(j):
        return pltpu.make_async_copy(hstage(j), ph_out.at[span((j // events) * hrows, hrows), span(lax.rem(j, events) * bw, bw)], pt_sem.at[odd(j)])

    def hblock(j):
        @pl.when(lax.rem(j, events) >= 2)
        def _():
            hstore(j - 2).wait()
        rows = span((j // events) * hrows, hrows)
        cols = span(lax.rem(j, events) * bw, bw)
        hstage(j)[:] = dotf(o_sib[rows, :], wpair[:qn, cols]) + dotf(sq[rows, :], wpair[qn:q2, cols]) + dotf(kvc[rows, :], wpair[q2:q2 + kw, cols])
        hstore(j).start()

    def final_y(dr, sub, acc):
        rows = span((2 * dr + sub) * pos, pos)
        y_v[rows, :] = (y_v[rows, :].astype(F32) + acc).astype(BF)

    def step_c(e):
        @pl.when(e == last)
        def _():
            first_sends(1)

        @pl.when(e >= 2)
        def _():
            serve(0, e, final_y)

        @pl.when(e == 0)
        def _():
            total(gown, b_s.at[0])
            total(gown, b_s.at[2])
            total(wqts_out, wq_r.at[0])
            total(wpair.at[lead(qn)], w_s.at[0])
            for c in ld2:
                c.start()
            d_rows[:] = jnp.zeros_like(d_rows)
            gn[:] = jnp.zeros_like(gn)
            qga[:] = jnp.zeros_like(qga)
            kga[:] = jnp.zeros_like(kga)

        paced(e, 2, units, 6, run_unit)

        @pl.when(e == 8)
        def _():
            kv_two(batch - 1)
        paced(e, 8, batch * tiles, 3, run_fold)

        @pl.when(e == 10)
        def _():
            each(0, events, settle)
            each(0, nz, lambda k: [swap(k, dr, kk).start() for dr in both for kk in both])

        @pl.when(e == 11)
        def _():
            for c in ld2:
                c.wait()
            total(sq, qs.at[1, 0])
            total(skv, qs.at[1, 1])
            each(0, nz, gather_h)
        paced(e, 11, events, 2, hblock)

        @pl.when(e == 12)
        def _():
            for j in (last, final_e):
                hstore(j).wait()
            first_fetch(1)

    each(0, events, step_c)

    def gblk(j):
        return qr.at[:, span(odd(j) * bw, bw)]

    def hblk(j):
        return gd.at[:, span(odd(j) * bw, bw)]

    def swo(j):
        return d_rows.at[lead(qn), span(odd(j) * bw, bw)]

    def swq(j):
        return d_rows.at[pl.ds(pl.multiple_of(qn + odd(j) * bw, bw), bw), lead(qn)]

    def g_load(j):
        return pltpu.make_async_copy(gy_out.at[:, span(j * bw, bw)], gblk(j), gls.at[odd(j)])

    def h_load(j):
        return pltpu.make_async_copy(hid.at[:, span(j * bw, bw)], hblk(j), hls.at[odd(j)])

    def wo_store(j):
        return pltpu.make_async_copy(swo(j), gwo_hbm.at[:, span(j * bw, bw)], swos.at[odd(j)])

    def wq_store(j):
        return pltpu.make_async_copy(swq(j), gq_hbm.at[span(j * bw, bw)], swqs.at[odd(j)])

    def block(j):
        g_load(j).wait()
        h_load(j).wait()

        @pl.when(j + 1 < events)
        def _():
            g_load(j + 1).start()
            h_load(j + 1).start()

        @pl.when(j >= 2)
        def _():
            wo_store(j - 2).wait()
            wq_store(j - 2).wait()
        cols = span(j * bw, bw)
        swo(j)[:] = dotf(o_own[:], gblk(j)[:], TN)
        ge_v[:, cols] = dotf(hotm[:], gblk(j)[:])
        wo_store(j).start()
        swq(j)[:] = dotf(hblk(j)[:], qt[:], TN)
        gkv_v[:, cols] = dotf(kvrow[:], hblk(j)[:], TN)[:kh]
        wq_store(j).start()

    def final_h(dr, sub, gh):
        rows = span((2 * dr + sub) * sub_rows, sub_rows)
        x = gown[rows, :].astype(F32)
        r = lax.rsqrt(row_mean(x * x) + EPS)
        ge_v[rows, :] += rms_pull(x, gh * gain[:], r)

    outs = [pltpu.make_async_copy(s, t, out_sem.at[i]) for i, (s, t) in enumerate((
        (y_v, y_hbm), (gkv_v.at[lead(kn)], gk_hbm), (gkv_v.at[pl.ds(kn, kn)], gv_hbm)))]

    def ge_store(dr, sub):
        rows = pl.ds((2 * dr + sub) * sub_rows, sub_rows)
        return pltpu.make_async_copy(ge_v.at[rows], ge_hbm.at[rows], out_sem.at[3])

    g_load(0).start()
    h_load(0).start()
    outs[0].start()
    work_d = events - 3

    wide = gn_out.shape[1]
    gtop = d // wide
    mrow = half(gtop)

    def to_sib(t):
        if t:
            return rdma(gfin.at[core], gfin.at[core], gs.at[4], gs.at[5], sib)
        return rdma(gmine.at[1 - core], gsib, gs.at[0], gs.at[1], sib)

    def to_col(k):
        return rdma(gcol.at[z], gcol.at[z], gs.at[2], gs.at[3], 2 * lax.rem(z + k, nz) + core)

    def step_d(e):
        @pl.when(e >= 2)
        def _():
            serve(1, e, final_h)

        @pl.when(e == 0)
        def _():
            for k in both:
                for c in item(k):
                    c.start()

        paced(e, 2, events, 4, lambda j: hblock(j + events))

        @pl.when(e == 5)
        def _():
            for j in (last, final_e):
                hstore(j + events).wait()
        paced(e, 2, events, 8, gain_part)
        paced(e, 5, events, work_d - 5, block)

        @pl.when(e == 10)
        def _():
            whole = jnp.sum(gn[:], axis=0, keepdims=True)
            for k, extra in ((0, qga), (1, kga)):
                for j in range(mrow):
                    c0 = (k * mrow + j) * wide
                    gmine[k, j:j + 1, :] = whole[:, c0:c0 + wide].astype(BF)
                gmine[k, mrow:mrow + 1, :] = extra[:].astype(BF)
            to_sib(0).start()

        @pl.when(e == 11)
        def _():
            total(gsib, gs.at[1])
            gcol[z] = (gmine[core].astype(F32) + gsib[:].astype(F32)).astype(BF)
            for k in range(1, nz):
                to_col(k).start()

        @pl.when(e == 13)
        def _():
            total(gcol.at[lead(nz - 1)], gs.at[3])
            gfin[core] = sum(gcol[k].astype(F32) for k in range(nz))
            to_sib(1).start()

        @pl.when(e == events - 3)
        def _():
            outs[1].start()
            outs[2].start()

        @pl.when(e == last)
        def _():
            for dr in both:
                ge_store(dr, 0).start()

    each(0, events, step_d)

    for dr in both:
        ge_store(dr, 1).start()
    for ph in both:
        for k in range(4):
            arrived(rs.at[ph, k])

    total(gy_out.at[lead(2 * (events - 4) * pos)], b_s.at[1])
    total(gy_out.at[lead(2 * (last) * pos)], b_s.at[3])
    to_far.wait_send()
    relay.wait_send()
    total(wpair.at[pl.ds(q2, kh)], w_s.at[2])
    total(o_sib, o_s.at[0])
    total(pk.at[lead(half(batch))], p1s.at[0])
    total(fk, p2s.at[0])
    total(sq, qs.at[0, 0])
    total(skv, qs.at[0, 1])
    total(gfin.at[0], gs.at[5])
    gn_out[:mrow] = gfin[0, :mrow]
    gn_out[mrow:] = gfin[1, :mrow]
    gqg_out[:] = gfin[0, mrow:mrow + 1, :]
    gkg_out[:] = gfin[1, mrow:mrow + 1, :]
    total(gsib, gs.at[0])
    total(gcol.at[lead(nz - 1)], gs.at[2])
    total(gfin.at[0], gs.at[4])
    for j in (last, final_e):
        wo_store(j).wait()
        wq_store(j).wait()
    total(ge_v, out_sem.at[3])
    for c in outs:
        c.wait()


def step_kernel(nz, embed, gy, wq, wk_t, wv_t, wo, gain, qg, kg, cos, sin_s, tok_seq):
    vrows, d = embed.shape
    vocab = vrows * 2 * nz
    qn, kn = wq.shape[1], wk_t.shape[0]
    hd = qg.shape[1]
    batch, seq = tok_seq.shape
    toks = batch * seq
    ev = 2 * nz
    kw, kh, q2, th = 4 * kn, 2 * kn, 2 * qn, toks // 2
    two = pltpu.SemaphoreType.DMA((2,))
    one = pltpu.SemaphoreType.DMA((1,))
    four = pltpu.SemaphoreType.DMA((4,))
    sr, hb, vh = vrows // 4, half(seq), half(vocab)
    mr = (d // half(hd) + 1 + 15) // 16 * 16
    dma = pltpu.SemaphoreType.DMA
    v = pltpu.VMEM

    def arr(dt, *shape):
        return jax.ShapeDtypeStruct(shape, dt)

    outs = (arr(BF, vrows, d), arr(F32, vrows, d), arr(F32, d, qn), arr(F32, kn, d), arr(F32, kn, d), arr(F32, qn, d), arr(F32, d // hd, hd), arr(F32, 1, hd), arr(F32, 1, hd), arr(BF, vh, d),
            arr(BF, vocab, d), arr(BF, toks, d), arr(BF, qn, d), arr(BF, qn, d), arr(F32, vh, d), arr(F32, vh, d))
    return pl.pallas_call(
        functools.partial(body, nz),
        name='step_kernel',
        out_shape=outs,
        in_specs=[ANY] * 6 + [VM] * 6,
        out_specs=(ANY,) * 6 + (VM,) * 3 + (ANY,) * 7,
        scratch_shapes=[v((vocab, d), BF), v((q2 + kw, d), BF), v((max(d, 2 * toks), qn), BF), v((vocab, qn), BF), v((toks, qn), BF), v((vh, qn), BF), v((vh, qn), BF),
                        v((toks, 2 * hd), BF), v((toks, hd), BF), v((2, th, kw), BF), v((2, th, kw), BF), v((vocab, kw), BF), v((vh, kw), BF), v((vh, kw), BF),
                        v((vocab, qn + kw), F32), v((4, 2, sr, d), F32), v((2, vrows, d), BF), v((vrows, d), BF), v((vrows, toks), BF),
                        v((seq, hd), F32), v((seq, hd), F32), v((batch, 4, hb, kw), BF), v((batch, 2, hb, kw), BF), v((batch, hb, kw), BF), v((batch, hb, kw), F32),
                        v((batch, hb, kw), BF), v((batch, seq, kw), BF), v((8, d), F32), v((1, hd), F32), v((1, hd), F32), v((2, mr, hd), BF), v((mr, hd), BF), v((nz, mr, hd), BF), v((2, mr, hd), F32), v((vrows, d), BF), v((vrows, d), F32), v((kh, d), F32),
                        dma((12,)), two, one, dma((ev,)), dma((ev,)), two, four, two, two, dma((2, 2)), one, four, two,
                        two, dma((2, 2)), dma((2, 4)), one, dma((batch,)), one, dma((batch,)), dma((2, 2)),
                        two, two, two, two, dma((6,)), four, dma((3,))],
        compiler_params=pltpu.CompilerParams(collective_id=0, has_side_effects=True, vmem_limit_bytes=67043328),
        cost_estimate=pl.CostEstimate(flops=2 * vocab * d * 8 * qn, bytes_accessed=20 * vocab * d, transcendentals=0),
    )(embed, gy, wq, wk_t, wv_t, wo, gain, qg, kg, cos, sin_s, tok_seq)


def emit_body(cuts, *refs):
    n = len(cuts)
    src, dst = refs[:n], refs[n:2 * n]
    bufs, s_in, s_out = refs[2 * n:-2], refs[-2], refs[-1]
    ins, outs = [], []
    for i, c in enumerate(cuts):
        step = src[i].shape[0] // c
        for j in range(c):
            b = bufs[i].at[pl.ds(j * step, step)]
            ins.append(pltpu.make_async_copy(src[i].at[pl.ds(j * step, step)], b, s_in.at[len(ins)]))
            outs.append(pltpu.make_async_copy(b, dst[i].at[pl.ds(j * step, step)], s_out.at[len(outs)]))
    for c in ins:
        c.start()
    for a, b in zip(ins, outs):
        a.wait()
        b.start()
    for b in outs:
        b.wait()


def emit(*arrays):
    size = 1 << 20
    cuts = tuple(max(1, a.size * a.dtype.itemsize // size) for a in arrays)
    return pl.pallas_call(
        functools.partial(emit_body, cuts),
        name='emit',
        out_shape=tuple(jax.ShapeDtypeStruct(a.shape, a.dtype) for a in arrays),
        in_specs=[ANY] * len(arrays),
        out_specs=(ANY,) * len(arrays),
        scratch_shapes=[pltpu.VMEM(a.shape, a.dtype) for a in arrays] + [pltpu.SemaphoreType.DMA((sum(cuts),))] * 2,
        compiler_params=pltpu.CompilerParams(vmem_limit_bytes=60 * 1024 * 1024),
        cost_estimate=pl.CostEstimate(flops=0, bytes_accessed=2 * sum(a.size * a.dtype.itemsize for a in arrays), transcendentals=0),
    )(*arrays)


def rope_consts(seq, hd):
    inv = np.float32(ROPE_BASE) ** (np.float32(-2.0) * np.arange(half(hd), dtype=np.float32) / np.float32(hd))
    ang = np.arange(seq, dtype=np.float32)[:, None] * inv.astype(np.float32)[None, :]
    ang = np.concatenate([ang, ang], axis=-1)
    sign = np.where(np.arange(hd) < half(hd), -1.0, 1.0).astype(np.float32)
    return np.cos(ang).astype(np.float32), (np.sin(ang) * sign).astype(np.float32)


def solution(mesh):
    tp = mesh.shape['tp']
    nz = tp // 2

    def local_step(tok_ids, embed_loc, norm_gain, q_gain, k_gain, wq, wk, wv, wo, gy_loc):
        d_model = embed_loc.shape[1]
        batch, seq = tok_ids.shape
        seq_dev = seq // tp
        hd = q_gain.shape[0]
        cos_c, sin_c = (jnp.asarray(t) for t in rope_consts(seq, hd))
        r = step_kernel(nz, embed_loc, gy_loc.reshape(batch * seq_dev, d_model), wq, wk.T, wv.T, wo, *(t[None, :] for t in (norm_gain, q_gain, k_gain)), cos_c, sin_c, tok_ids)
        y, g_embed, g_wq, g_wk, g_wv, g_wo, g_n, g_q, g_k = emit(*r[:9])
        return (y.reshape(batch, seq_dev, d_model), g_embed, g_n.reshape(d_model), g_q.reshape(hd), g_k.reshape(hd), g_wq, g_wk.T, g_wv.T, g_wo)

    cols = P(None, 'tp')
    in_specs = (P('dp', None), P('tp', None), P(), P(), P(), cols, cols, cols, P('tp', None), P('dp', 'tp', None))
    out_specs = (P('dp', 'tp', None), P(('dp', 'tp'), None), P('dp'), P('dp'), P('dp'), P('dp', 'tp'), P('dp', 'tp'), P('dp', 'tp'), P(('dp', 'tp'), None))
    return jax.shard_map(local_step, mesh=mesh, in_specs=in_specs, out_specs=out_specs, check_vma=False)
```

time: 356 us -> 358 us (level)
  no operation moved by 1% of the time
where the time goes in v1:
time: 358 us
  Pallas kernels  357 us (100%)
    pallas_call x1, Pallas kernels, step_kernel(): pl.pallas_call(functools.partial(body, nz), name='step_kernel', out_shape...  342 us
    pallas_call x1, Pallas kernels, emit(): pl.pallas_call(functools.partial(emit_body, cuts), name='emit', out_shape...  14.8 us

profile of v1, /device:TPU:21, one launch (start us, length us, event | category | flops | bytes accessed | tf_op | source)
XLA Modules:
  0.0 358.1 jit_solution(2785149661529215728)
XLA Ops:
  0.6 342.4 %step_kernel.1 = (bf16[128,4096]{1,0:T(8,128)(2,1)}, f32[128,4096]{1,0:T(8,128)}, f32[4096,512]{1,0:T(8,128)}, f32[32,4096]{1,0:T(8,128)}, f32[32,4096]{1,0:T(8,...) custom-call(bf16[128,4096]{1,0:T(8,128)(2,1)} %embed.1, ...), custom_call_target="tpu_custom_call" | custom-call | flops 68719476736 | bytes 167772160 | tf_op jit(solution)/shard_map/step_kernel/pallas_call | solution.py:953
  343.1 14.8 %emit.1 = (bf16[128,4096]{1,0:T(8,128)(2,1)}, f32[128,4096]{1,0:T(8,128)}, f32[4096,512]{1,0:T(8,128)}, f32[32,4096]{1,0:T(8,128)}, f32[32,4096]{1,0:T(8,128)}, ...) custom-call(bf16[128,4096]{1,0:T(8,128)(2,1)} %get-tuple-element.27.refs_0_, ...), custom_call_target="tpu_custom_call" | custom-call | bytes 41977856 | tf_op jit(solution)/shard_map/emit/pallas_call | solution.py:995
